TPU v7x, 8 devices: a whole 2x2x1 slice. The times are simulated.
8 devices in a mesh: dp: 1 (over z), tp: 8 (over y, x, core).
Axes of the slice: x: 2, y: 2, z: 1, core: 2. Of those that a mesh axis runs over, the one named last changes fastest.
Arguments:
- hidden: bfloat16 [1, 8192, 4096], P('dp', 'tp')
- attn_gain: float32 [4096], replicated
- attn_bias: float32 [4096], replicated
- mlp_gain: float32 [4096], replicated
- mlp_bias: float32 [4096], replicated
- w_qkv: bfloat16 [4096, 8, 768], P(None, 'tp')
- w_out: bfloat16 [4096, 4096], P('tp')
- w_up: bfloat16 [4096, 16384], P(None, 'tp')
- w_down: bfloat16 [16384, 4096], P('tp')
- positions: int32 [8192], replicated
Outputs:
- output: bfloat16 [1, 8192, 4096], P('dp', 'tp')
All inputs are finite; a program needn't handle non-finite values.
Results may differ from a plain program's by a relative error of at most 0.00473784.
Values are sent between devices in bfloat16 or wider.
A program may use at most 1 GiB of HBM per device.

v0:
```python
import jax
import jax.numpy as jnp
from jax import lax
from jax.sharding import PartitionSpec as P


def layer_norm(tok_rows, norm_gain, norm_bias):
    rows32 = tok_rows.astype(jnp.float32)
    row_mean = jnp.mean(rows32, axis=-1, keepdims=True)
    centered = rows32 - row_mean
    row_var = jnp.mean(centered * centered, axis=-1, keepdims=True)
    return (centered * lax.rsqrt(row_var + 1e-5) * norm_gain + norm_bias).astype(jnp.bfloat16)


def rotary_tables(positions, head_dim):
    inv_freq = 10000.0 ** (-2.0 * jnp.arange(head_dim // 2, dtype=jnp.float32) / head_dim)
    angles = positions.astype(jnp.float32)[:, None] * inv_freq[None, :]
    angles = jnp.concatenate([angles, angles], axis=-1)
    return jnp.cos(angles), jnp.sin(angles)


def apply_rotary(head_vals, cos_tab, sin_tab):
    half_dim = head_vals.shape[-1] // 2
    vals32 = head_vals.astype(jnp.float32)
    rotated = jnp.concatenate([-vals32[..., half_dim:], vals32[..., :half_dim]], axis=-1)
    return (vals32 * cos_tab + rotated * sin_tab).astype(jnp.bfloat16)


def attention_branch(normed, w_qkv_part, w_out_part, positions):
    batch_size, seq_len, model_width = normed.shape
    num_groups = w_qkv_part.shape[1]
    slot_cols = w_qkv_part.shape[2]
    group_cols = w_out_part.shape[0] // num_groups
    head_dim = (slot_cols - group_cols) // 2
    group_size = group_cols // head_dim
    qkv_rows = jnp.einsum('bsd,dkc->bskc', normed, w_qkv_part, preferred_element_type=jnp.float32).astype(jnp.bfloat16)
    qkv_rows = qkv_rows.reshape(batch_size, seq_len, num_groups, group_size + 2, head_dim)
    cos_tab, sin_tab = rotary_tables(positions, head_dim)
    query_rot = apply_rotary(qkv_rows[:, :, :, :group_size, :], cos_tab[None, :, None, None, :], sin_tab[None, :, None, None, :])
    key_rot = apply_rotary(qkv_rows[:, :, :, group_size, :], cos_tab[None, :, None, :], sin_tab[None, :, None, :])
    value_seq = qkv_rows[:, :, :, group_size + 1, :]
    block_len = min(seq_len, 256)
    num_blocks = seq_len // block_len
    key_idx = jnp.arange(seq_len)
    score_scale = head_dim ** -0.5

    def one_block(block_idx):
        row_start = block_idx * block_len
        query_blk = lax.dynamic_slice_in_dim(query_rot, row_start, block_len, axis=1)
        scores = jnp.einsum('bqkgh,bskh->bkgqs', query_blk, key_rot, preferred_element_type=jnp.float32) * score_scale
        query_idx = row_start + jnp.arange(block_len)
        allowed = key_idx[None, :] <= query_idx[:, None]
        scores = jnp.where(allowed, scores, -1e30)
        exp_scores = jnp.exp(scores - jnp.max(scores, axis=-1, keepdims=True))
        attn_probs = (exp_scores / jnp.sum(exp_scores, axis=-1, keepdims=True)).astype(jnp.bfloat16)
        context = jnp.einsum('bkgqs,bskh->bqkgh', attn_probs, value_seq, preferred_element_type=jnp.float32)
        return context.astype(jnp.bfloat16).reshape(batch_size, block_len, num_groups * group_cols)

    ctx_blocks = lax.map(one_block, jnp.arange(num_blocks))
    attn_part = jnp.einsum('nbqc,cd->bnqd', ctx_blocks, w_out_part, preferred_element_type=jnp.float32)
    return attn_part.reshape(batch_size, seq_len, model_width)


def solution(mesh):
    def local_layer(hidden_blk, attn_gain, attn_bias, mlp_gain, mlp_bias, w_qkv_part, w_out_part, w_up_part, w_down_part, positions):
        normed_attn = layer_norm(hidden_blk, attn_gain, attn_bias)
        normed_mlp = layer_norm(hidden_blk, mlp_gain, mlp_bias)
        attn_in = lax.all_gather(normed_attn, 'tp', axis=1, tiled=True)
        mlp_in = lax.all_gather(normed_mlp, 'tp', axis=1, tiled=True)
        attn_part = attention_branch(attn_in, w_qkv_part, w_out_part, positions)
        up_pre = jnp.einsum('bsd,df->bsf', mlp_in, w_up_part, preferred_element_type=jnp.float32)
        up_act = jax.nn.gelu(up_pre, approximate=False).astype(jnp.bfloat16)
        mlp_part = jnp.einsum('bsf,fd->bsd', up_act, w_down_part, preferred_element_type=jnp.float32)
        token_sum = lax.psum_scatter(attn_part + mlp_part, 'tp', scatter_dimension=1, tiled=True)
        return (hidden_blk.astype(jnp.float32) + token_sum).astype(jnp.bfloat16)

    return jax.shard_map(local_layer, mesh=mesh, in_specs=(P('dp', 'tp', None), P(), P(), P(), P(), P(None, 'tp', None), P('tp', None), P(None, 'tp'), P('tp', None), P()), out_specs=P('dp', 'tp', None), check_vma=False)
```

profile of v0, /device:TPU:0, one launch (start us, length us, event | category | flops | bytes accessed | tf_op | source)
XLA Modules:
  0.0 3285.1 jit_solution(9513039346297350169)
XLA Ops:
  43.2 283.1 %all-gather.3.cloned.1.call-done = bf16[1,8192,4096]{2,1,0:T(8,128)(2,1)} async-done(((bf16[1,1024,4096]{2,1,0:T(8,128)(2,1)}), bf16[1,8192,4096]{2,1,0:T(8,128)(2,1)}) %all-gather.3.cloned.1.call-update) | async-done | bytes 67108880 | tf_op jit(solution)/shard_map/all_gather | solution.py:68
  326.3 60.5 %fusion.48 = bf16[8192,768]{0,1:T(8,128)(2,1)} fusion(bf16[1,8192,4096]{2,1,0:T(8,128)(2,1)} %all-gather.3.cloned.1.call-done, bf16[4096,1,768]{2,0,1:T(8,128)(2,1)} %param.17), kind=kOutput, calls=%fused_computation.61 | convolution fusion | flops 51545899008 | bytes 85983232 | tf_op jit(solution)/shard_map/bsd,dkc->bskc/dot_general | solution.py:36
  402.5 17.1 fusion.60
  440.9 1598.2 %while.11 = (s32[]{:T(128)}, bf16[32,1,256,512]{2,3,1,0:T(8,128)(2,1)}, s32[32]{0:T(128)S(1)}, bf16[1,8192,1,4,128]{1,4,3,2,0:T(8,128)(2,1)}, bf16[1,8192,1,128]...) while((s32[]{:T(128)}, ...), condition=%wide.region_5.6_spmd.clone, body=%wide.region_2.5_spmd.clone.sunk | while | flops 4397856768 | bytes 114317496 | solution.py:59
  443.5 15.8 fusion.75
  543.4 15.8 fusion.75
  593.4 15.8 fusion.75
  693.2 15.8 fusion.75
  743.2 15.8 fusion.75
  793.1 15.8 fusion.75
  843.1 15.8 fusion.75
  893.0 15.8 fusion.75
  943.0 15.8 fusion.75
  1042.8 15.8 fusion.75
  1092.8 15.8 fusion.75
  1142.7 15.8 fusion.75
  1192.7 15.8 fusion.75
  1242.6 15.8 fusion.75
  1492.3 15.8 fusion.75
  1542.2 15.8 fusion.75
  1592.2 15.8 fusion.75
  1642.1 15.8 fusion.75
  1692.1 15.8 fusion.75
  1742.0 15.8 fusion.75
  1791.9 15.8 fusion.75
  1891.8 15.8 fusion.75
  1941.8 15.8 fusion.75
  1991.7 15.8 fusion.75
  2039.1 53.1 %fusion.51 = f32[32,256,4096]{2,1,0:T(8,128)} fusion(bf16[32,1,256,512]{2,3,1,0:T(8,128)(2,1)} %get-tuple-element.42, bf16[512,4096]{1,0:T(8,128)(2,1)} %param.18), kind=kOutput, calls=%fused_computation.64 | convolution fusion | flops 34359738368 | bytes 146800640 | tf_op jit(solution)/shard_map/nbqc,cd->bnqd/dot_general | solution.py:60
  2092.2 288.5 %fusion.22 = bf16[8192,2048]{1,0:T(8,128)(2,1)} fusion(bf16[4096,2048]{1,0:T(8,128)(2,1)} %param.19, bf16[1,8192,4096]{2,1,0:T(8,128)(2,1)} %all-gather.5.cloned.1.call-done), kind=kOutput, calls=%fused_computation.25 | convolution fusion | flops 138529472512 | bytes 117440512 | tf_op jit(solution)/shard_map/bsd,df->bsf/dot_general | solution.py:71
  2380.7 153.6 %fusion.19 = f32[1,8192,4096]{2,1,0:T(8,128)} fusion(bf16[8192,2048]{1,0:T(8,128)(2,1)} %fusion.22, bf16[2048,4096]{1,0:T(8,128)(2,1)} %param.20, f32[32,256,4096]{2,1,0:T(8,128)} %fusion.51), kind=kOutput, calls=%fused_computation.22 | convolution fusion | flops 137472507904 | bytes 318767104 | tf_op jit(solution)/shard_map/bsf,fd->bsd/dot_general | solution.py:73
  2534.3 732.0 %reduce-scatter.2.cloned.1.call-done = f32[1,1024,4096]{2,1,0:T(8,128)} async-done(((f32[1,8192,4096]{2,1,0:T(8,128)}), f32[1,1024,4096]{2,1,0:T(8,128)}) %reduce-scatter.2.cloned.1.call-update) | async-done | bytes 16777232 | tf_op jit(solution)/shard_map/reduce_scatter | solution.py:74
  (242 shorter events, 1282.4 us)
Async XLA Ops:
  6.5 10.6 copy-start.4
  6.5 10.6 copy-start.5
  6.5 10.7 copy-start.2
  6.5 10.7 copy-start.3
  6.5 319.7 %all-gather.3.cloned.1.call-start = ((), (), s32[]{:S(2)}) async-start(), calls=%async_computation.1 | async-start | bytes 75497472 | tf_op jit(solution)/shard_map/all_gather | solution.py:68
  6.6 10.6 slice-start
  11.3 5.9 slice-start.1
  17.2 9.8 copy-start.1
  26.1 2066.2 %all-gather.5.cloned.1.call-start = ((), (), s32[]{:S(2)}) async-start(), calls=%async_computation.2 | async-start | bytes 75497472 | tf_op jit(solution)/shard_map/all_gather | solution.py:69
  26.8 3239.5 %reduce-scatter.2.cloned.1.call-start = ((), (), s32[]{:S(2)}) async-start(), calls=%async_computation.3 | async-start | bytes 150994944 | tf_op jit(solution)/shard_map/reduce_scatter | solution.py:74
  423.7 7.0 copy-start
Sparse Core Ops, SparseCore 0:
  26.2 300.0 all-gather.2
  328.1 297.1 all-gather.4
  2534.5 731.8 reduce-scatter.1
where the time goes:
time: 3290 us
  matrix products  1570 us (48%)
  waiting for transfers between devices  1020 us (31%)
  other arithmetic  621 us (19%)
  local copies, waits for them, and re-layouts  47.3 us (1%)
    reduce_scatter x1, waiting for transfers between devices, local_layer(): lax.psum_scatter(attn_part + mlp_part, 'tp', scatter_dimension=1, tiled=T...  732 us
    dot_general x32, matrix products, one_block(): jnp.einsum('bqkgh,bskh->bkgqs', query_blk, key_rot, preferred_element_typ...  506 us
    dot_general x32, matrix products, one_block(): jnp.einsum('bkgqs,bskh->bqkgh', attn_probs, value_seq, preferred_element_...  504 us
    reduce_sum x32, other arithmetic, one_block(): jnp.sum(exp_scores, axis=-1, keepdims=True)  482 us
    dot_general x1, matrix products, local_layer(): jnp.einsum('bsd,df->bsf', mlp_in, w_up_part, preferred_element_type=jnp.f...  288 us
    all_gather x1, waiting for transfers between devices, local_layer(): attn_in = lax.all_gather(normed_attn, 'tp', axis=1, tiled=True)  283 us
    dot_general x1, matrix products, local_layer(): jnp.einsum('bsf,fd->bsd', up_act, w_down_part, preferred_element_type=jnp...  154 us
  transfers between devices with their start and end apart: 3, of which 2 were waited for; matrix products, arithmetic and copies ran while one was open for 54% of the time, Pallas kernels for 0%

commit v1 on v0

v1 whole, which is shorter than its diff:
```python
import functools

import jax
import jax.numpy as jnp
from jax import lax
from jax.experimental import pallas as pl
from jax.experimental.pallas import tpu as pltpu
from jax.sharding import PartitionSpec as P


CHUNKS = 4
KV_BLOCK = 512
HEAD = 128
LOG2E = 1.4426950408889634
NORM_ROWS = 16
TILE = 256


def norm_kernel(core_ref, x_ref, ag_ref, ab_ref, mg_ref, mb_ref, a_ref, m_ref):
    width = x_ref.shape[-1]

    def group(i, carry):
        rows = pl.ds(pl.multiple_of(i * NORM_ROWS, NORM_ROWS), NORM_ROWS)
        tiles = [x_ref[rows, t * 512:(t + 1) * 512].astype(jnp.float32) for t in range(width // 512)]
        mean = jnp.sum(functools.reduce(jnp.add, tiles), axis=-1, keepdims=True) * (1.0 / width)
        tiles = [tile - mean for tile in tiles]
        var = jnp.sum(functools.reduce(jnp.add, [tile * tile for tile in tiles]), axis=-1, keepdims=True) * (1.0 / width)
        inv = lax.rsqrt(var + 1e-5)
        for t, tile in enumerate(tiles):
            cols = slice(t * 512, (t + 1) * 512)
            unit = tile * inv
            a_ref[rows, cols] = (unit * ag_ref[:, cols] + ab_ref[:, cols]).astype(jnp.bfloat16)
            m_ref[rows, cols] = (unit * mg_ref[:, cols] + mb_ref[:, cols]).astype(jnp.bfloat16)
        return carry

    lax.fori_loop(0, x_ref.shape[0] // NORM_ROWS, group, 0, unroll=2)


def two_norms(core, rows, blk, attn_gain, attn_bias, mlp_gain, mlp_bias):
    num_rows, width = rows.shape
    sub = min(blk, 256)
    per = blk // sub
    chips = num_rows // (2 * blk)

    def source(i, core_ref):
        half = i // (chips * per)
        chip = (i // per) % chips
        dev = 2 * chip + jnp.where(half == 0, 1 - core_ref[0], core_ref[0])
        return (dev * per + i % per, 0)

    vec = pl.BlockSpec((1, width), lambda i, core_ref: (0, 0))
    out = pl.BlockSpec((sub, width), lambda i, core_ref: (i, 0))
    return pl.pallas_call(
        norm_kernel,
        grid_spec=pltpu.PrefetchScalarGridSpec(
            num_scalar_prefetch=1,
            grid=(num_rows // sub,),
            in_specs=[pl.BlockSpec((sub, width), source), vec, vec, vec, vec],
            out_specs=[out, out],
        ),
        out_shape=[jax.ShapeDtypeStruct((num_rows, width), jnp.bfloat16)] * 2,
        cost_estimate=pl.CostEstimate(flops=num_rows * width * 500, bytes_accessed=num_rows * width * 6, transcendentals=0),
        name="two_norms",
    )(core, rows, attn_gain[None], attn_bias[None], mlp_gain[None], mlp_bias[None])


def rotate_kernel(x_ref, cos_ref, sin_ref, q_ref, k_ref):
    cos_tab, sin_tab = cos_ref[...], sin_ref[...]
    q_heads = q_ref.shape[1] // HEAD
    for h in range(q_heads + 1):
        vals32 = x_ref[:, h * HEAD:(h + 1) * HEAD].astype(jnp.float32)
        turned = (vals32 * cos_tab + pltpu.roll(vals32, HEAD // 2, 1) * sin_tab).astype(jnp.bfloat16)
        if h < q_heads:
            q_ref[:, h * HEAD:(h + 1) * HEAD] = turned
        else:
            k_ref[...] = turned


def rotate(qkv, cos_tab, sin_tab):
    num_rows, cols = qkv.shape
    q_cols = cols - 2 * HEAD
    sub = min(num_rows, 256)

    def spec(c):
        return pl.BlockSpec((sub, c), lambda i: (i, 0))

    return pl.pallas_call(
        rotate_kernel,
        grid=(num_rows // sub,),
        in_specs=[spec(cols), spec(HEAD), spec(HEAD)],
        out_specs=[spec(q_cols), spec(HEAD)],
        out_shape=[jax.ShapeDtypeStruct((num_rows, q_cols), jnp.bfloat16), jax.ShapeDtypeStruct((num_rows, HEAD), jnp.bfloat16)],
        cost_estimate=pl.CostEstimate(flops=num_rows * cols * 500, bytes_accessed=num_rows * cols * 5, transcendentals=0),
        name="rotate",
    )(qkv, cos_tab, sin_tab)


def up_gelu_kernel(x_ref, w_ref, o_ref):
    spots = [(r, c) for c in range(0, o_ref.shape[1], TILE) for r in range(0, o_ref.shape[0], TILE)]

    def pre(r, c):
        return jnp.dot(x_ref[r:r + TILE, :], w_ref[:, c:c + TILE], preferred_element_type=jnp.float32)

    held = pre(*spots[0])
    for n, (r, c) in enumerate(spots):
        ahead = pre(*spots[n + 1]) if n + 1 < len(spots) else None
        o_ref[r:r + TILE, c:c + TILE] = (0.5 * held * (1.0 + lax.erf(held * 0.7071067811865476))).astype(jnp.bfloat16)
        held = ahead


def up_gelu(rows, w_up):
    num_rows, width = rows.shape
    cols = w_up.shape[1]
    sub, wide = min(num_rows, 1024), min(cols, 512)
    return pl.pallas_call(
        up_gelu_kernel,
        grid=(num_rows // sub, cols // wide),
        in_specs=[pl.BlockSpec((sub, width), lambda i, j: (i, 0)), pl.BlockSpec((width, wide), lambda i, j: (0, j))],
        out_specs=pl.BlockSpec((sub, wide), lambda i, j: (i, j)),
        out_shape=jax.ShapeDtypeStruct((num_rows, cols), jnp.bfloat16),
        cost_estimate=pl.CostEstimate(flops=2 * num_rows * width * cols, bytes_accessed=2 * num_rows * (width + cols) + 4 * width * cols, transcendentals=0),
        name="up_gelu",
    )(rows, w_up)


def project_kernel(ctx_ref, up_ref, wo_ref, wd_ref, *rest):
    o_ref = rest[-1]
    for c in range(0, o_ref.shape[1], TILE):
        for r in range(0, o_ref.shape[0], TILE):
            total = jnp.dot(ctx_ref[r:r + TILE, :], wo_ref[:, c:c + TILE], preferred_element_type=jnp.float32)
            total += jnp.dot(up_ref[r:r + TILE, :], wd_ref[:, c:c + TILE], preferred_element_type=jnp.float32)
            if len(rest) == 2:
                total += rest[0][r:r + TILE, c:c + TILE].astype(jnp.float32)
            o_ref[r:r + TILE, c:c + TILE] = total.astype(o_ref.dtype)


def project(context, up_rows, w_out, w_down, half, num_rows, part, parts, take, dtype):
    cols = w_out.shape[1] // parts
    wide = min(cols, 512)
    first = part * (cols // wide)
    depth = w_out.shape[0] + w_down.shape[0]
    in_specs = [
        pl.BlockSpec((num_rows, context.shape[1]), lambda j: (half, 0)),
        pl.BlockSpec((num_rows, up_rows.shape[1]), lambda j: (half, 0)),
        pl.BlockSpec((w_out.shape[0], wide), lambda j: (0, first + j)),
        pl.BlockSpec((w_down.shape[0], wide), lambda j: (0, first + j)),
    ]
    args = [context, up_rows, w_out, w_down]
    out_spec = pl.BlockSpec((num_rows, wide), lambda j: (0, j))
    if take is not None:
        in_specs.append(out_spec)
        args.append(take)
    return pl.pallas_call(
        project_kernel,
        grid=(cols // wide,),
        in_specs=in_specs,
        out_specs=out_spec,
        out_shape=jax.ShapeDtypeStruct((num_rows, cols), dtype),
        cost_estimate=pl.CostEstimate(flops=2 * num_rows * depth * cols, bytes_accessed=2 * depth * (num_rows + cols) + 4 * num_rows * cols, transcendentals=0),
        name="project",
    )(*args)


def attend_kernel(group, q_blk, seg, offset, chips, core_ref, q_ref, k_ref, v_ref, o_ref, m_ref, l_ref, acc_ref):
    i = pl.program_id(0)
    half = i // chips
    dev = 2 * (i % chips) + jnp.where(half == 0, 1 - core_ref[0], core_ref[0])
    row_start = dev * seg + offset
    scale = HEAD ** -0.5 * LOG2E
    m_ref[...] = jnp.full(m_ref.shape, -1e30, jnp.float32)
    l_ref[...] = jnp.zeros(l_ref.shape, jnp.float32)
    acc_ref[...] = jnp.zeros(acc_ref.shape, jnp.float32)
    lanes = KV_BLOCK // HEAD

    def block(col_start, masked):
        cols = pl.ds(pl.multiple_of(col_start, KV_BLOCK), KV_BLOCK)
        key_blk = k_ref[cols, :]
        value_blk = v_ref[cols, :]
        if masked:
            row_idx = row_start + lax.broadcasted_iota(jnp.int32, (q_blk, KV_BLOCK), 0)
            col_idx = col_start + lax.broadcasted_iota(jnp.int32, (q_blk, KV_BLOCK), 1)
            allowed = col_idx <= row_idx

        def score(h):
            query = q_ref[:, h * HEAD:(h + 1) * HEAD]
            scores = lax.dot_general(query, key_blk, (((1,), (1,)), ((), ())), preferred_element_type=jnp.float32)
            return jnp.where(allowed, scores, -1e30) if masked else scores

        def weigh(h, scores):
            m_prev = m_ref[h]
            m_next = jnp.maximum(m_prev, jnp.max(scores, axis=1, keepdims=True))
            m_ref[h] = m_next
            alpha = jnp.exp2((m_prev - m_next) * scale)
            probs = [jnp.exp2((scores[:, t * HEAD:(t + 1) * HEAD] - m_next) * scale) for t in range(lanes)]
            l_ref[h] = alpha * l_ref[h] + functools.reduce(jnp.add, probs)
            return alpha, jnp.concatenate([p.astype(jnp.bfloat16) for p in probs], axis=1)

        def gather_values(h, alpha, prob_blk):
            acc_ref[h] = alpha * acc_ref[h] + jnp.dot(prob_blk, value_blk, preferred_element_type=jnp.float32)

        scores = score(0)
        held = None
        for h in range(group):
            ahead = score(h + 1) if h + 1 < group else None
            now = weigh(h, scores)
            if held is not None:
                gather_values(h - 1, *held)
            held, scores = now, ahead
        gather_values(group - 1, *held)

    full = row_start // KV_BLOCK

    def step(j, carry):
        block(j * KV_BLOCK, False)
        return carry

    lax.fori_loop(0, full, step, 0)
    block(full * KV_BLOCK, True)
    for h in range(group):
        total = jnp.sum(l_ref[h], axis=1, keepdims=True)
        o_ref[:, h * HEAD:(h + 1) * HEAD] = (acc_ref[h] / total).astype(jnp.bfloat16)


def attend(core, q_rows, keys, values, q_blk, seg, offset):
    num_rows, q_cols = q_rows.shape
    seq_len = keys.shape[0]
    group = q_cols // HEAD
    chips = num_rows // (2 * q_blk)
    row_spec = pl.BlockSpec((q_blk, q_cols), lambda i, core_ref: (i, 0))
    kv_spec = pl.BlockSpec((seq_len, HEAD), lambda i, core_ref: (0, 0))
    stat = pltpu.VMEM((group, q_blk, HEAD), jnp.float32)
    return pl.pallas_call(
        functools.partial(attend_kernel, group, q_blk, seg, offset, chips),
        grid_spec=pltpu.PrefetchScalarGridSpec(
            num_scalar_prefetch=1,
            grid=(num_rows // q_blk,),
            in_specs=[row_spec, kv_spec, kv_spec],
            out_specs=row_spec,
            scratch_shapes=[stat, stat, stat],
        ),
        out_shape=jax.ShapeDtypeStruct((num_rows, q_cols), jnp.bfloat16),
        cost_estimate=pl.CostEstimate(
            flops=num_rows * seq_len * q_cols * 8, bytes_accessed=num_rows * q_cols * 4 + seq_len * HEAD * 4, transcendentals=num_rows * seq_len * group // 2
        ),
        name="attend",
    )(core, q_rows, keys, values)


def rotary_tables(positions):
    inv_freq = 10000.0 ** (-2.0 * jnp.arange(HEAD // 2, dtype=jnp.float32) / HEAD)
    angles = positions.astype(jnp.float32)[:, None] * inv_freq[None, :]
    cos_half, sin_half = jnp.cos(angles), jnp.sin(angles)
    return jnp.concatenate([cos_half, cos_half], axis=-1), jnp.concatenate([-sin_half, sin_half], axis=-1)


def solution(mesh):
    tp = mesh.shape['tp']
    chips = tp // 2

    def swap(bits):
        return [(d, d ^ bits) for d in range(tp)]

    def dot32(left, right):
        return jnp.dot(left, right, preferred_element_type=jnp.float32)

    def local_layer(hidden_blk, attn_gain, attn_bias, mlp_gain, mlp_bias, w_qkv_part, w_out_part, w_up_part, w_down_part, positions):
        me = lax.axis_index('tp')
        core_bit = me % 2
        chip = me // 2
        core = core_bit.astype(jnp.int32)[None]
        seg, width = hidden_blk.shape[1:]
        blk = seg // CHUNKS
        x_rows = hidden_blk[0]
        w_qkv_flat = w_qkv_part[:, 0, :]
        group_cols = w_out_part.shape[0]

        cos_tab, sin_tab = rotary_tables(positions)

        def own_order(table):
            table = table.reshape(chips, 2, CHUNKS, blk, HEAD)
            table = jnp.where(core_bit == 0, table[:, ::-1], table)
            return table.transpose(2, 1, 0, 3, 4).reshape(CHUNKS, tp * blk, HEAD)

        cos_own, sin_own = own_order(cos_tab), own_order(sin_tab)

        gathered = [lax.all_gather(x_rows[c * blk:(c + 1) * blk], 'tp', axis=0, tiled=True) for c in range(CHUNKS)]
        queries, keys, values, ups = [], [], [], []
        prev = None
        for c in range(CHUNKS):
            rows = gathered[c]
            if prev is not None:
                rows, ups[-1] = lax.optimization_barrier((rows, prev))
            normed_attn, normed_mlp = two_norms(core, rows, blk, attn_gain, attn_bias, mlp_gain, mlp_bias)
            qkv = dot32(normed_attn, w_qkv_flat).astype(jnp.bfloat16)
            query, key = rotate(qkv, cos_own[c], sin_own[c])
            queries.append(query)
            keys.append(key)
            values.append(qkv[:, group_cols + HEAD:])
            prev = up_gelu(normed_mlp, w_up_part)
            ups.append(prev)

        def device_major(parts):
            stacked = jnp.stack(parts).reshape(CHUNKS, 2, chips, blk, HEAD)
            stacked = jnp.where(core_bit == 0, stacked[:, ::-1], stacked)
            return stacked.transpose(2, 1, 0, 3, 4).reshape(tp * seg, HEAD)

        all_keys, all_values = device_major(keys), device_major(values)

        half = chips * blk

        def partner(give):
            return lax.ppermute(give, 'tp', swap(1))

        def split(keep, c, cols):
            pair = keep.reshape(chips, blk, keep.shape[1])
            own = x_rows[c * blk:(c + 1) * blk, cols].astype(jnp.float32) + lax.dynamic_index_in_dim(pair, chip, 0, keepdims=False)
            return own, [lax.dynamic_index_in_dim(pair, chip ^ flip, 0, keepdims=False).astype(jnp.bfloat16) for flip in range(1, chips)]

        def send(own, away):
            for flip, block in zip(range(1, chips), away):
                moved = lax.ppermute(block, 'tp', swap(2 * flip))
                own = own + moved.astype(jnp.float32)
            return own.astype(jnp.bfloat16)

        def attended(c):
            return attend(core, queries[c], all_keys, all_values, blk, seg, c * blk)

        def give_rows(context, c, part, parts):
            return project(context, ups[c], w_out_part, w_down_part, 0, half, part, parts, None, jnp.bfloat16)

        def keep_rows(context, c, part, parts, take):
            return project(context, ups[c], w_out_part, w_down_part, 1, half, part, parts, take, jnp.float32)

        outs = []
        every = slice(0, width)
        ready = None
        for c in range(CHUNKS - 1):
            context = attended(c)
            if ready is not None:
                outs.append(send(*ready))
            give = give_rows(context, c, 0, 1)
            if c > 0:
                queries[c + 1], give = lax.optimization_barrier((queries[c + 1], give))
            ready = split(keep_rows(context, c, 0, 1, partner(give)), c, every)
            if c == 0:
                queries[1], ready = lax.optimization_barrier((queries[1], ready))
        c = CHUNKS - 1
        context = attended(c)
        outs.append(send(*ready))
        takes = [partner(give_rows(context, c, part, 2)) for part in range(2)]
        tails = []
        for part in range(2):
            cols = slice(part * (width // 2), (part + 1) * (width // 2))
            ready = split(keep_rows(context, c, part, 2, takes[part]), c, cols)
            if part == 0:
                ready, takes[1] = lax.optimization_barrier((ready, takes[1]))
            tails.append(send(*ready))
        outs.append(jnp.concatenate(tails, axis=1))
        return jnp.concatenate(outs)[None]

    return jax.shard_map(local_layer, mesh=mesh, in_specs=(P('dp', 'tp', None), P(), P(), P(), P(), P(None, 'tp', None), P('tp', None), P(None, 'tp'), P('tp', None), P()), out_specs=P('dp', 'tp', None), check_vma=False)
```

time: 3290 us -> 1340 us (0.41)
  matrix products: 1570 us -> 72.4 us
  Pallas kernels: 0 us -> 811 us
  waiting for transfers between devices: 1020 us -> 286 us
  other arithmetic: 621 us -> 87.7 us
    dot_general x68 -> x4, matrix products: 1570 us -> 72.4 us  [dot32(): return jnp.dot(left, right, preferred_element_type=jnp.float32)]
    pallas_call x0 -> x26, Pallas kernels: none -> 811 us  [the longest x4 264 us: attend(): pl.pallas_call(functools.partial(attend_kernel, group, q_blk, seg, offset...]
    reduce_scatter x1 -> x0, waiting for transfers between devices: 732 us -> none  [local_layer(): lax.psum_scatter(attn_part + mlp_part, 'tp', scatter_dimension=1, tiled=T...]
    reduce_sum x34 -> x0, other arithmetic: 493 us -> none  [the longest x32 482 us: one_block(): jnp.sum(exp_scores, axis=-1, keepdims=True)]
    ppermute x0 -> x20, waiting for transfers between devices: none -> 219 us  [the longest x15 219 us: send(): moved = lax.ppermute(block, 'tp', swap(2 * flip))]
    all_gather x2 -> x4, waiting for transfers between devices: 283 us -> 64.9 us  [local_layer(): lax.all_gather(x_rows[c * blk:(c + 1) * blk], 'tp', axis=0, tiled=True)]
    convert_element_type x5 -> x4, other arithmetic: 59.4 us -> 17 us  [send(): return own.astype(jnp.bfloat16)]
    le x32 -> x0, other arithmetic: 40.9 us -> none  [one_block(): allowed = key_idx[None, :] <= query_idx[:, None]]
  transfers between devices with their start and end apart: 3 -> 24, of which waited for: 2 -> 12; matrix products, arithmetic and copies ran while one was open for 54% -> 10% of each run, Pallas kernels for 0% -> 34%
where the time goes in v1:
time: 1340 us; the launch traced here: 1330 us
  Pallas kernels  811 us (61%)
  waiting for transfers between devices  286 us (21%)
  other arithmetic  87.7 us (7%)
  matrix products  72.4 us (5%)
  local copies, waits for them, and re-layouts  45.3 us (3%)
  starting transfers between devices  16.8 us (1%)
  between operations  13.7 us (1%)
    pallas_call x4, Pallas kernels, attend(): pl.pallas_call(functools.partial(attend_kernel, group, q_blk, seg, offset...  264 us
    pallas_call x10, Pallas kernels, project(): pl.pallas_call(project_kernel, grid=(cols // wide,), in_specs=in_specs, o...  236 us
    ppermute x15, waiting for transfers between devices, send(): moved = lax.ppermute(block, 'tp', swap(2 * flip))  219 us
    pallas_call x4, Pallas kernels, up_gelu(): pl.pallas_call(up_gelu_kernel, grid=(num_rows // sub, cols // wide), in_s...  177 us
    pallas_call x4, Pallas kernels, two_norms(): pl.pallas_call(norm_kernel, grid_spec=pltpu.PrefetchScalarGridSpec(num_sc...  105 us
    dot_general x4, matrix products, dot32(): return jnp.dot(left, right, preferred_element_type=jnp.float32)  72.4 us
    all_gather x4, waiting for transfers between devices, local_layer(): lax.all_gather(x_rows[c * blk:(c + 1) * blk], 'tp', axis=0, tiled=True)  64.9 us
    convert_element_type x5, local copies, waits for them, and re-layouts, split(): lax.dynamic_index_in_dim(pair, chip ^ flip, 0, keepdims=False)  32.7 us
  transfers between devices with their start and end apart: 24, of which 12 were waited for; matrix products, arithmetic and copies ran while one was open for 10% of the time, Pallas kernels for 34%

profile of v1, /device:TPU:0, one launch (start us, length us, event | category | flops | bytes accessed | tf_op | source)
XLA Modules:
  0.0 1332.8 jit_solution(13847793428206180443)
XLA Ops:
  14.7 17.4 %fusion.41 = (f32[4,2,4,256,64]{4,3,0,1,2:T(8,128)}, f32[4,2,4,256,64]{4,3,0,1,2:T(8,128)}, f32[4,2,4,256,64]{4,3,0,1,2:T(8,128)}) fusion(f32[64]{0:T(128)S(1)} %multiply_power_fusion, f32[4,2,4,256]{3,0,1,2:T(4,128)S(1)} %copy.19), kind=kLoop, calls=%fused_computation.66 | loop fusion | flops 1048576 | bytes 6324480 | tf_op jit(solution)/shard_map/neg | solution.py:253
  51.2 48.6 %all-gather.11.cloned.1.call-done = bf16[1,2048,4096]{2,1,0:T(8,128)(2,1)} async-done(((bf16[1,256,4096]{2,1,0:T(8,128)(2,1)}), bf16[1,2048,4096]{2,1,0:T(8,128)(2,1)}) %all-gather.11.cloned.1.call-update) | async-done | bytes 16777232 | tf_op jit(solution)/shard_map/all_gather | solution.py:286
  99.8 26.1 %two_norms.4 = (bf16[2048,4096]{1,0:T(8,128)(2,1)}, bf16[2048,4096]{1,0:T(8,128)(2,1)}) custom-call(s32[1]{0:T(128)} %bitcast.core_ref, bf16[2048,4096]{1,0:T(8,128)(2,1)} %bitcast.135, f32[1,4096]{1,0:T(1,128)} %bitcast.166, f32[1,4096]{1,0:T(1,128)} %bitcast.170, f32[1,4096]{1,0:T(1,128)} %bitcast.174, f32[1,4096]{1,0:T(1,128)} %bitcast.178), custom_call_target="tpu_custom_call" | custom-call | flops 4194304000 | bytes 50331648 | tf_op jit(solution)/shard_map/two_norms/pallas_call | solution.py:53
  125.9 43.7 %up_gelu.4.up_ref = bf16[2048,2048]{1,0:T(8,128)(2,1)} custom-call(bf16[2048,4096]{1,0:T(8,128)(2,1)} %get-tuple-element.41.x_ref, bf16[4096,2048]{1,0:T(8,128)(2,1)} %w_ref.7), custom_call_target="tpu_custom_call" | custom-call | flops 34359738368 | bytes 58720256 | tf_op jit(solution)/shard_map/up_gelu/pallas_call | solution.py:115
  185.9 18.0 %fusion.19.x_ref = bf16[2048,768]{1,0:T(8,128)(2,1)S(1)} fusion(bf16[2048,4096]{1,0:T(8,128)(2,1)} %get-tuple-element.45, bf16[4096,1,768]{2,0,1:T(8,128)(2,1)} %param.15), kind=kOutput, calls=%fused_computation.37 | convolution fusion | flops 12886474752 | bytes 26214400 | tf_op jit(solution)/shard_map/dot_general | solution.py:264
  205.6 26.7 %two_norms.5 = (bf16[2048,4096]{1,0:T(8,128)(2,1)}, bf16[2048,4096]{1,0:T(8,128)(2,1)}) custom-call(s32[1]{0:T(128)} %bitcast.core_ref, bf16[2048,4096]{1,0:T(8,128)(2,1)} %bitcast.134, f32[1,4096]{1,0:T(1,128)} %bitcast.167, f32[1,4096]{1,0:T(1,128)} %bitcast.171, f32[1,4096]{1,0:T(1,128)} %bitcast.175, f32[1,4096]{1,0:T(1,128)} %bitcast.179), custom_call_target="tpu_custom_call" | custom-call | flops 4194304000 | bytes 50331648 | tf_op jit(solution)/shard_map/two_norms/pallas_call | solution.py:53
  232.3 18.0 %fusion.16.x_ref = bf16[2048,768]{1,0:T(8,128)(2,1)S(1)} fusion(bf16[2048,4096]{1,0:T(8,128)(2,1)} %get-tuple-element.43, bf16[4096,1,768]{2,0,1:T(8,128)(2,1)} %param.15), kind=kOutput, calls=%fused_computation.36 | convolution fusion | flops 12886474752 | bytes 26214400 | tf_op jit(solution)/shard_map/dot_general | solution.py:264
  250.3 44.9 %up_gelu.5.up_ref = bf16[2048,2048]{1,0:T(8,128)(2,1)} custom-call(bf16[2048,4096]{1,0:T(8,128)(2,1)} %get-tuple-element.49.x_ref, bf16[4096,2048]{1,0:T(8,128)(2,1)} %w_ref.7), custom_call_target="tpu_custom_call" | custom-call | flops 34359738368 | bytes 58720256 | tf_op jit(solution)/shard_map/up_gelu/pallas_call | solution.py:115
  295.2 26.2 %two_norms.6 = (bf16[2048,4096]{1,0:T(8,128)(2,1)}, bf16[2048,4096]{1,0:T(8,128)(2,1)}) custom-call(s32[1]{0:T(128)} %bitcast.core_ref, bf16[2048,4096]{1,0:T(8,128)(2,1)} %bitcast.133, f32[1,4096]{1,0:T(1,128)} %bitcast.168, f32[1,4096]{1,0:T(1,128)} %bitcast.172, f32[1,4096]{1,0:T(1,128)} %bitcast.176, f32[1,4096]{1,0:T(1,128)} %bitcast.180), custom_call_target="tpu_custom_call" | custom-call | flops 4194304000 | bytes 50331648 | tf_op jit(solution)/shard_map/two_norms/pallas_call | solution.py:53
  321.4 18.3 %fusion.22.x_ref = bf16[2048,768]{1,0:T(8,128)(2,1)S(1)} fusion(bf16[2048,4096]{1,0:T(8,128)(2,1)} %get-tuple-element.51, bf16[4096,1,768]{2,0,1:T(8,128)(2,1)} %param.15), kind=kOutput, calls=%fused_computation.38 | convolution fusion | flops 12886474752 | bytes 26214400 | tf_op jit(solution)/shard_map/dot_general | solution.py:264
  339.7 44.7 %up_gelu.6.up_ref = bf16[2048,2048]{1,0:T(8,128)(2,1)} custom-call(bf16[2048,4096]{1,0:T(8,128)(2,1)} %get-tuple-element.53.x_ref, bf16[4096,2048]{1,0:T(8,128)(2,1)} %w_ref.7), custom_call_target="tpu_custom_call" | custom-call | flops 34359738368 | bytes 58720256 | tf_op jit(solution)/shard_map/up_gelu/pallas_call | solution.py:115
  384.5 26.0 %two_norms.7 = (bf16[2048,4096]{1,0:T(8,128)(2,1)}, bf16[2048,4096]{1,0:T(8,128)(2,1)}) custom-call(s32[1]{0:T(128)} %bitcast.core_ref, bf16[2048,4096]{1,0:T(8,128)(2,1)} %bitcast.132, f32[1,4096]{1,0:T(1,128)} %bitcast.169, f32[1,4096]{1,0:T(1,128)} %bitcast.173, f32[1,4096]{1,0:T(1,128)} %bitcast.177, f32[1,4096]{1,0:T(1,128)} %bitcast.181), custom_call_target="tpu_custom_call" | custom-call | flops 4194304000 | bytes 50331648 | tf_op jit(solution)/shard_map/two_norms/pallas_call | solution.py:53
  410.4 18.1 %fusion.25.x_ref = bf16[2048,768]{1,0:T(8,128)(2,1)S(1)} fusion(bf16[2048,4096]{1,0:T(8,128)(2,1)} %get-tuple-element.55, bf16[4096,1,768]{2,0,1:T(8,128)(2,1)} %param.15), kind=kOutput, calls=%fused_computation.39 | convolution fusion | flops 12886474752 | bytes 26214400 | tf_op jit(solution)/shard_map/dot_general | solution.py:264
  463.0 62.5 %attend.4.ctx_ref = bf16[2048,512]{1,0:T(8,128)(2,1)} custom-call(s32[1]{0:T(128)} %bitcast.core_ref, bf16[2048,512]{1,0:T(8,128)(2,1)} %get-tuple-element.46.q_ref, bf16[8192,128]{1,0:T(8,128)(2,1)} %bitcast.154, bf16[8192,128]{1,0:T(8,128)(2,1)} %bitcast.158), custom_call_target="tpu_custom_call" | custom-call | flops 68719476736 | bytes 8388608 | tf_op jit(solution)/shard_map/attend/pallas_call | solution.py:232
  525.4 27.7 %project.10 = bf16[1024,4096]{1,0:T(8,128)(2,1)} custom-call(bf16[2048,512]{1,0:T(8,128)(2,1)} %attend.4.ctx_ref, bf16[2048,2048]{1,0:T(8,128)(2,1)} %up_gelu.4.up_ref, bf16[512,4096]{1,0:T(8,128)(2,1)} %wo_ref.19, bf16[2048,4096]{1,0:T(8,128)(2,1)} %wd_ref.19), custom_call_target="tpu_custom_call" | custom-call | flops 21474836480 | bytes 42991616 | tf_op jit(solution)/shard_map/project/pallas_call | solution.py:153
  553.8 43.6 %up_gelu.7.up_ref = bf16[2048,2048]{1,0:T(8,128)(2,1)} custom-call(bf16[2048,4096]{1,0:T(8,128)(2,1)} %get-tuple-element.71.x_ref, bf16[4096,2048]{1,0:T(8,128)(2,1)} %w_ref.7), custom_call_target="tpu_custom_call" | custom-call | flops 34359738368 | bytes 58720256 | tf_op jit(solution)/shard_map/up_gelu/pallas_call | solution.py:115
  597.4 28.8 %project.11 = f32[1024,4096]{1,0:T(8,128)} custom-call(bf16[2048,512]{1,0:T(8,128)(2,1)} %attend.4.ctx_ref, bf16[2048,2048]{1,0:T(8,128)(2,1)} %up_gelu.4.up_ref, bf16[512,4096]{1,0:T(8,128)(2,1)} %wo_ref.19, bf16[2048,4096]{1,0:T(8,128)(2,1)} %wd_ref.19, bf16[1024,4096]{1,0:T(8,128)(2,1)} %collective-permute-done.rest_0_), custom_call_target="tpu_custom_call" | custom-call | flops 21474836480 | bytes 42991616 | tf_op jit(solution)/shard_map/project/pallas_call | solution.py:153
  639.5 62.5 %attend.5.ctx_ref = bf16[2048,512]{1,0:T(8,128)(2,1)} custom-call(s32[1]{0:T(128)} %bitcast.core_ref, bf16[2048,512]{1,0:T(8,128)(2,1)} %get-tuple-element.62.q_ref, bf16[8192,128]{1,0:T(8,128)(2,1)} %bitcast.155, bf16[8192,128]{1,0:T(8,128)(2,1)} %bitcast.159), custom_call_target="tpu_custom_call" | custom-call | flops 68719476736 | bytes 8388608 | tf_op jit(solution)/shard_map/attend/pallas_call | solution.py:232
  701.9 27.9 %project.12 = bf16[1024,4096]{1,0:T(8,128)(2,1)} custom-call(bf16[2048,512]{1,0:T(8,128)(2,1)} %attend.5.ctx_ref, bf16[2048,2048]{1,0:T(8,128)(2,1)} %up_gelu.5.up_ref, bf16[512,4096]{1,0:T(8,128)(2,1)} %wo_ref.19, bf16[2048,4096]{1,0:T(8,128)(2,1)} %wd_ref.19), custom_call_target="tpu_custom_call" | custom-call | flops 21474836480 | bytes 42991616 | tf_op jit(solution)/shard_map/project/pallas_call | solution.py:153
  729.8 69.7 %attend.6.ctx_ref = bf16[2048,512]{1,0:T(8,128)(2,1)} custom-call(s32[1]{0:T(128)} %bitcast.core_ref, bf16[2048,512]{1,0:T(8,128)(2,1)} %get-tuple-element.66.q_ref, bf16[8192,128]{1,0:T(8,128)(2,1)} %bitcast.156, bf16[8192,128]{1,0:T(8,128)(2,1)} %bitcast.160), custom_call_target="tpu_custom_call" | custom-call | flops 68719476736 | bytes 8388608 | tf_op jit(solution)/shard_map/attend/pallas_call | solution.py:232
  799.5 27.5 %project.14 = bf16[1024,4096]{1,0:T(8,128)(2,1)} custom-call(bf16[2048,512]{1,0:T(8,128)(2,1)} %attend.6.ctx_ref, bf16[2048,2048]{1,0:T(8,128)(2,1)} %up_gelu.6.up_ref, bf16[512,4096]{1,0:T(8,128)(2,1)} %wo_ref.19, bf16[2048,4096]{1,0:T(8,128)(2,1)} %wd_ref.19), custom_call_target="tpu_custom_call" | custom-call | flops 21474836480 | bytes 42991616 | tf_op jit(solution)/shard_map/project/pallas_call | solution.py:153
  827.0 69.7 %attend.7.ctx_ref = bf16[2048,512]{1,0:T(8,128)(2,1)} custom-call(s32[1]{0:T(128)} %bitcast.core_ref, bf16[2048,512]{1,0:T(8,128)(2,1)} %get-tuple-element.70.q_ref, bf16[8192,128]{1,0:T(8,128)(2,1)} %bitcast.157, bf16[8192,128]{1,0:T(8,128)(2,1)} %bitcast.161), custom_call_target="tpu_custom_call" | custom-call | flops 68719476736 | bytes 8388608 | tf_op jit(solution)/shard_map/attend/pallas_call | solution.py:232
  931.5 17.4 %project.17 = f32[1024,2048]{1,0:T(8,128)} custom-call(bf16[2048,512]{1,0:T(8,128)(2,1)} %attend.7.ctx_ref, bf16[2048,2048]{1,0:T(8,128)(2,1)} %up_gelu.7.up_ref, bf16[512,4096]{1,0:T(8,128)(2,1)} %wo_ref.19, bf16[2048,4096]{1,0:T(8,128)(2,1)} %wd_ref.19, bf16[1024,2048]{1,0:T(8,128)(2,1)} %collective-permute-done.12.rest_0_), custom_call_target="tpu_custom_call" | custom-call | flops 10737418240 | bytes 24117248 | tf_op jit(solution)/shard_map/project/pallas_call | solution.py:153
  981.2 28.8 %project.15 = f32[1024,4096]{1,0:T(8,128)} custom-call(bf16[2048,512]{1,0:T(8,128)(2,1)} %attend.6.ctx_ref, bf16[2048,2048]{1,0:T(8,128)(2,1)} %up_gelu.6.up_ref, bf16[512,4096]{1,0:T(8,128)(2,1)} %wo_ref.19, bf16[2048,4096]{1,0:T(8,128)(2,1)} %wd_ref.19, bf16[1024,4096]{1,0:T(8,128)(2,1)} %collective-permute-done.8.rest_0_), custom_call_target="tpu_custom_call" | custom-call | flops 21474836480 | bytes 42991616 | tf_op jit(solution)/shard_map/project/pallas_call | solution.py:153
  1025.3 20.3 %collective-permute-done.14 = bf16[256,2048]{1,0:T(8,128)(2,1)S(1)} collective-permute-done((bf16[256,2048]{1,0:T(8,128)(2,1)}, bf16[256,2048]{1,0:T(8,128)(2,1)S(1)}, u32[]{:S(2)}, u32[]{:S(2)}) %collective-permute-start.14) | collective-permute-done | bytes 1048608 | tf_op jit(solution)/shard_map/ppermute | solution.py:321
  1047.1 22.1 %collective-permute-done.15 = bf16[256,2048]{1,0:T(8,128)(2,1)} collective-permute-done((bf16[256,2048]{1,0:T(8,128)(2,1)}, bf16[256,2048]{1,0:T(8,128)(2,1)}, u32[]{:S(2)}, u32[]{:S(2)}) %collective-permute-start.15) | collective-permute-done | bytes 1048608 | tf_op jit(solution)/shard_map/ppermute | solution.py:321
  1069.2 29.1 %project.13 = f32[1024,4096]{1,0:T(8,128)} custom-call(bf16[2048,512]{1,0:T(8,128)(2,1)} %attend.5.ctx_ref, bf16[2048,2048]{1,0:T(8,128)(2,1)} %up_gelu.5.up_ref, bf16[512,4096]{1,0:T(8,128)(2,1)} %wo_ref.19, bf16[2048,4096]{1,0:T(8,128)(2,1)} %wd_ref.19, bf16[1024,4096]{1,0:T(8,128)(2,1)} %collective-permute-done.4.rest_0_), custom_call_target="tpu_custom_call" | custom-call | flops 21474836480 | bytes 42991616 | tf_op jit(solution)/shard_map/project/pallas_call | solution.py:153
  1116.1 42.0 %collective-permute-done.9 = bf16[256,4096]{1,0:T(8,128)(2,1)} collective-permute-done((bf16[256,4096]{1,0:T(8,128)(2,1)}, bf16[256,4096]{1,0:T(8,128)(2,1)}, u32[]{:S(2)}, u32[]{:S(2)}) %collective-permute-start.9) | collective-permute-done | bytes 2097184 | tf_op jit(solution)/shard_map/ppermute | solution.py:321
  1168.4 34.7 %collective-permute-done.11 = bf16[256,4096]{1,0:T(8,128)(2,1)S(1)} collective-permute-done((bf16[256,4096]{1,0:T(8,128)(2,1)}, bf16[256,4096]{1,0:T(8,128)(2,1)S(1)}, u32[]{:S(2)}, u32[]{:S(2)}) %collective-permute-start.11) | collective-permute-done | bytes 2097184 | tf_op jit(solution)/shard_map/ppermute | solution.py:321
  1203.8 44.3 %collective-permute-done.5 = bf16[256,4096]{1,0:T(8,128)(2,1)} collective-permute-done((bf16[256,4096]{1,0:T(8,128)(2,1)}, bf16[256,4096]{1,0:T(8,128)(2,1)}, u32[]{:S(2)}, u32[]{:S(2)}) %collective-permute-start.5) | collective-permute-done | bytes 2097184 | tf_op jit(solution)/shard_map/ppermute | solution.py:321
  1248.1 44.4 %collective-permute-done.7 = bf16[256,4096]{1,0:T(8,128)(2,1)} collective-permute-done((bf16[256,4096]{1,0:T(8,128)(2,1)}, bf16[256,4096]{1,0:T(8,128)(2,1)}, u32[]{:S(2)}, u32[]{:S(2)}) %collective-permute-start.7) | collective-permute-done | bytes 2097184 | tf_op jit(solution)/shard_map/ppermute | solution.py:321
  1300.6 25.4 %maximum_bitcast_fusion = bf16[1,1024,4096]{2,1,0:T(8,128)(2,1)} fusion(bf16[256,2048]{1,0:T(8,128)(2,1)S(1)} %fusion.40, bf16[256,2048]{1,0:T(8,128)(2,1)S(1)} %add_convert_fusion.1, bf16[256,4096]{1,0:T(8,128)(2,1)S(1)} %get-tuple-element.87, bf16[256,4096]{1,0:T(8,128)(2,1)S(1)} %get-tuple-element.86, bf16[256,4096]{1,0:T(8,128)(2,1)S(1)} %add_convert_fusion), kind=kLoop, calls=%fused_computation | loop fusion | flops 41943040 | bytes 16777216 | tf_op jit(solution)/shard_map/broadcast_in_dim | solution.py:359
  (110 shorter events, 214.0 us)
Async XLA Ops:
  6.5 93.3 %all-gather.11.cloned.1.call-start = ((), (), s32[]{:S(2)}) async-start(), calls=%async_computation.1 | async-start | bytes 18874368 | tf_op jit(solution)/shard_map/all_gather | solution.py:286
  12.5 173.3 %all-gather.9.cloned.1.call-start = ((), (), s32[]{:S(2)}) async-start(), calls=%async_computation | async-start | bytes 18874368 | tf_op jit(solution)/shard_map/all_gather | solution.py:286
  13.3 281.9 %all-gather.13.cloned.1.call-start = ((), (), s32[]{:S(2)}) async-start(), calls=%async_computation.2 | async-start | bytes 18874368 | tf_op jit(solution)/shard_map/all_gather | solution.py:286
  14.0 370.4 %all-gather.15.cloned.1.call-start = ((), (), s32[]{:S(2)}) async-start(), calls=%async_computation.3 | async-start | bytes 18874368 | tf_op jit(solution)/shard_map/all_gather | solution.py:286
  250.3 44.9 %copy-start.2 = (bf16[2048,768]{1,0:T(8,128)(2,1)}, bf16[2048,768]{1,0:T(8,128)(2,1)S(1)}, u32[]{:S(2)}) copy-start(bf16[2048,768]{1,0:T(8,128)(2,1)S(1)} %fusion.16.x_ref) | copy-start | bytes 9437188
  339.7 44.7 %copy-start.3 = (bf16[2048,768]{1,0:T(8,128)(2,1)}, bf16[2048,768]{1,0:T(8,128)(2,1)S(1)}, u32[]{:S(2)}) copy-start(bf16[2048,768]{1,0:T(8,128)(2,1)S(1)} %fusion.22.x_ref) | copy-start | bytes 9437188
  428.5 14.5 %copy-start.4 = (bf16[2048,768]{1,0:T(8,128)(2,1)}, bf16[2048,768]{1,0:T(8,128)(2,1)S(1)}, u32[]{:S(2)}) copy-start(bf16[2048,768]{1,0:T(8,128)(2,1)S(1)} %fusion.25.x_ref) | copy-start | bytes 9437188
  443.0 14.1 %copy-start.5 = (bf16[2048,128]{1,0:T(8,128)(2,1)S(1)}, bf16[2048,128]{1,0:T(8,128)(2,1)}, u32[]{:S(2)}) copy-start(bf16[2048,128]{1,0:T(8,128)(2,1)} %get-tuple-element.47) | copy-start | bytes 1572868
  443.0 14.1 %copy-start.6 = (bf16[2048,128]{1,0:T(8,128)(2,1)S(1)}, bf16[2048,128]{1,0:T(8,128)(2,1)}, u32[]{:S(2)}) copy-start(bf16[2048,128]{1,0:T(8,128)(2,1)} %get-tuple-element.48) | copy-start | bytes 1572868
  553.1 44.3 %collective-permute-start = (bf16[1024,4096]{1,0:T(8,128)(2,1)}, bf16[1024,4096]{1,0:T(8,128)(2,1)}, u32[]{:S(2)}, u32[]{:S(2)}) collective-permute-start(bf16[1024,4096]{1,0:T(8,128)(2,1)} %project.10), channel_id=1, source_target_pairs={{0,1},{1,0},{2,3},{3,2},{4,5},{5,4},{6,7},{7,6}} | collective-permute-start | bytes 25165832 | tf_op jit(solution)/shard_map/ppermute | solution.py:312
  827.0 153.6 %collective-permute-start.8 = (bf16[1024,4096]{1,0:T(8,128)(2,1)}, bf16[1024,4096]{1,0:T(8,128)(2,1)}, u32[]{:S(2)}, u32[]{:S(2)}) collective-permute-start(bf16[1024,4096]{1,0:T(8,128)(2,1)} %project.14), channel_id=1, source_target_pairs={{0,1},{1,0},{2,3},{3,2},{4,5},{5,4},{6,7},{7,6}} | collective-permute-start | bytes 25165832 | tf_op jit(solution)/shard_map/ppermute | solution.py:312
  912.6 18.3 %collective-permute-start.12 = (bf16[1024,2048]{1,0:T(8,128)(2,1)}, bf16[1024,2048]{1,0:T(8,128)(2,1)}, u32[]{:S(2)}, u32[]{:S(2)}) collective-permute-start(bf16[1024,2048]{1,0:T(8,128)(2,1)} %project.16), channel_id=1, source_target_pairs={{0,1},{1,0},{2,3},{3,2},{4,5},{5,4},{6,7},{7,6}} | collective-permute-start | bytes 12582920 | tf_op jit(solution)/shard_map/ppermute | solution.py:312
  913.1 156.1 %collective-permute-start.4 = (bf16[1024,4096]{1,0:T(8,128)(2,1)}, bf16[1024,4096]{1,0:T(8,128)(2,1)}, u32[]{:S(2)}, u32[]{:S(2)}) collective-permute-start(bf16[1024,4096]{1,0:T(8,128)(2,1)} %project.12), channel_id=1, source_target_pairs={{0,1},{1,0},{2,3},{3,2},{4,5},{5,4},{6,7},{7,6}} | collective-permute-start | bytes 25165832 | tf_op jit(solution)/shard_map/ppermute | solution.py:312
  928.9 26.8 %collective-permute-start.13 = (bf16[1024,2048]{1,0:T(8,128)(2,1)}, bf16[1024,2048]{1,0:T(8,128)(2,1)}, u32[]{:S(2)}, u32[]{:S(2)}) collective-permute-start(bf16[1024,2048]{1,0:T(8,128)(2,1)} %project.18), channel_id=1, source_target_pairs={{0,1},{1,0},{2,3},{3,2},{4,5},{5,4},{6,7},{7,6}} | collective-permute-start | bytes 12582920 | tf_op jit(solution)/shard_map/ppermute | solution.py:312
  929.4 49.7 %collective-permute-start.1 = (bf16[256,4096]{1,0:T(8,128)(2,1)}, bf16[256,4096]{1,0:T(8,128)(2,1)}, u32[]{:S(2)}, u32[]{:S(2)}) collective-permute-start(bf16[256,4096]{1,0:T(8,128)(2,1)} %get-tuple-element.59), channel_id=1, source_target_pairs={{0,2},{1,3},{2,0},{3,1},{4,6},{5,7},{6,4},{7,5}} | collective-permute-start | bytes 6291464 | tf_op jit(solution)/shard_map/ppermute | solution.py:321
  930.9 93.3 %collective-permute-start.2 = (bf16[256,4096]{1,0:T(8,128)(2,1)}, bf16[256,4096]{1,0:T(8,128)(2,1)}, u32[]{:S(2)}, u32[]{:S(2)}) collective-permute-start(bf16[256,4096]{1,0:T(8,128)(2,1)} %get-tuple-element.60), channel_id=1, source_target_pairs={{0,4},{1,5},{2,6},{3,7},{4,0},{5,1},{6,2},{7,3}} | collective-permute-start | bytes 6291464 | tf_op jit(solution)/shard_map/ppermute | solution.py:321
  955.7 68.5 %collective-permute-start.3 = (bf16[256,4096]{1,0:T(8,128)(2,1)}, bf16[256,4096]{1,0:T(8,128)(2,1)}, u32[]{:S(2)}, u32[]{:S(2)}) collective-permute-start(bf16[256,4096]{1,0:T(8,128)(2,1)} %get-tuple-element.61), channel_id=1, source_target_pairs={{0,6},{1,7},{2,4},{3,5},{4,2},{5,3},{6,0},{7,1}} | collective-permute-start | bytes 6291464 | tf_op jit(solution)/shard_map/ppermute | solution.py:321
  979.1 66.5 %collective-permute-start.14 = (bf16[256,2048]{1,0:T(8,128)(2,1)}, bf16[256,2048]{1,0:T(8,128)(2,1)S(1)}, u32[]{:S(2)}, u32[]{:S(2)}) collective-permute-start(bf16[256,2048]{1,0:T(8,128)(2,1)} %get-tuple-element.73), channel_id=1, source_target_pairs={{0,2},{1,3},{2,0},{3,1},{4,6},{5,7},{6,4},{7,5}} | collective-permute-start | bytes 3145736 | tf_op jit(solution)/shard_map/ppermute | solution.py:321
  980.6 88.6 %collective-permute-start.15 = (bf16[256,2048]{1,0:T(8,128)(2,1)}, bf16[256,2048]{1,0:T(8,128)(2,1)}, u32[]{:S(2)}, u32[]{:S(2)}) collective-permute-start(bf16[256,2048]{1,0:T(8,128)(2,1)} %get-tuple-element.74), channel_id=1, source_target_pairs={{0,4},{1,5},{2,6},{3,7},{4,0},{5,1},{6,2},{7,3}} | collective-permute-start | bytes 3145736 | tf_op jit(solution)/shard_map/ppermute | solution.py:321
  1024.3 82.2 %collective-permute-start.16 = (bf16[256,2048]{1,0:T(8,128)(2,1)}, bf16[256,2048]{1,0:T(8,128)(2,1)}, u32[]{:S(2)}, u32[]{:S(2)}) collective-permute-start(bf16[256,2048]{1,0:T(8,128)(2,1)} %get-tuple-element.75), channel_id=1, source_target_pairs={{0,6},{1,7},{2,4},{3,5},{4,2},{5,3},{6,0},{7,1}} | collective-permute-start | bytes 3145736 | tf_op jit(solution)/shard_map/ppermute | solution.py:321
  1024.3 85.7 %collective-permute-start.17 = (bf16[256,2048]{1,0:T(8,128)(2,1)}, bf16[256,2048]{1,0:T(8,128)(2,1)}, u32[]{:S(2)}, u32[]{:S(2)}) collective-permute-start(bf16[256,2048]{1,0:T(8,128)(2,1)} %get-tuple-element.88), channel_id=1, source_target_pairs={{0,2},{1,3},{2,0},{3,1},{4,6},{5,7},{6,4},{7,5}} | collective-permute-start | bytes 3145736 | tf_op jit(solution)/shard_map/ppermute | solution.py:321
  1045.6 67.7 %collective-permute-start.19 = (bf16[256,2048]{1,0:T(8,128)(2,1)}, bf16[256,2048]{1,0:T(8,128)(2,1)}, u32[]{:S(2)}, u32[]{:S(2)}) collective-permute-start(bf16[256,2048]{1,0:T(8,128)(2,1)} %get-tuple-element.89), channel_id=1, source_target_pairs={{0,6},{1,7},{2,4},{3,5},{4,2},{5,3},{6,0},{7,1}} | collective-permute-start | bytes 3145736 | tf_op jit(solution)/shard_map/ppermute | solution.py:321
  1069.2 45.6 %collective-permute-start.18 = (bf16[256,2048]{1,0:T(8,128)(2,1)}, bf16[256,2048]{1,0:T(8,128)(2,1)}, u32[]{:S(2)}, u32[]{:S(2)}) collective-permute-start(bf16[256,2048]{1,0:T(8,128)(2,1)} %get-tuple-element.90), channel_id=1, source_target_pairs={{0,4},{1,5},{2,6},{3,7},{4,0},{5,1},{6,2},{7,3}} | collective-permute-start | bytes 3145736 | tf_op jit(solution)/shard_map/ppermute | solution.py:321
  1069.2 89.0 %collective-permute-start.9 = (bf16[256,4096]{1,0:T(8,128)(2,1)}, bf16[256,4096]{1,0:T(8,128)(2,1)}, u32[]{:S(2)}, u32[]{:S(2)}) collective-permute-start(bf16[256,4096]{1,0:T(8,128)(2,1)} %get-tuple-element.80), channel_id=1, source_target_pairs={{0,2},{1,3},{2,0},{3,1},{4,6},{5,7},{6,4},{7,5}} | collective-permute-start | bytes 6291464 | tf_op jit(solution)/shard_map/ppermute | solution.py:321
  1098.2 60.5 %copy-start = (f32[256,4096]{1,0:T(8,128)S(1)}, f32[256,4096]{1,0:T(8,128)}, u32[]{:S(2)}) copy-start(f32[256,4096]{1,0:T(8,128)} %add_bitcast_fusion) | copy-start | bytes 12582916
  1098.3 64.6 %slice-start = ((s8[8388608]{0:T(1024)(128)(4,1)}), s8[4194304]{0:T(1024)(128)(4,1)S(1)}, s32[]{:S(2)}) async-start(s8[8388608]{0:T(1024)(128)(4,1)} %bitcast.125), calls=%async_computation.4 | async-start | bytes 8388608
  1106.5 96.6 %collective-permute-start.11 = (bf16[256,4096]{1,0:T(8,128)(2,1)}, bf16[256,4096]{1,0:T(8,128)(2,1)S(1)}, u32[]{:S(2)}, u32[]{:S(2)}) collective-permute-start(bf16[256,4096]{1,0:T(8,128)(2,1)} %get-tuple-element.81), channel_id=1, source_target_pairs={{0,6},{1,7},{2,4},{3,5},{4,2},{5,3},{6,0},{7,1}} | collective-permute-start | bytes 6291464 | tf_op jit(solution)/shard_map/ppermute | solution.py:321
  1110.0 52.9 %slice-start.1 = ((s8[8388608]{0:T(1024)(128)(4,1)}), s8[4194304]{0:T(1024)(128)(4,1)S(1)}, s32[]{:S(2)}) async-start(s8[8388608]{0:T(1024)(128)(4,1)} %bitcast.125), calls=%async_computation.5 | async-start | bytes 8388608
  1110.0 93.8 %collective-permute-start.10 = (bf16[256,4096]{1,0:T(8,128)(2,1)}, bf16[256,4096]{1,0:T(8,128)(2,1)S(1)}, u32[]{:S(2)}, u32[]{:S(2)}) collective-permute-start(bf16[256,4096]{1,0:T(8,128)(2,1)} %get-tuple-element.82), channel_id=1, source_target_pairs={{0,4},{1,5},{2,6},{3,7},{4,0},{5,1},{6,2},{7,3}} | collective-permute-start | bytes 6291464 | tf_op jit(solution)/shard_map/ppermute | solution.py:321
  1113.3 134.8 %collective-permute-start.5 = (bf16[256,4096]{1,0:T(8,128)(2,1)}, bf16[256,4096]{1,0:T(8,128)(2,1)}, u32[]{:S(2)}, u32[]{:S(2)}) collective-permute-start(bf16[256,4096]{1,0:T(8,128)(2,1)} %get-tuple-element.77), channel_id=1, source_target_pairs={{0,2},{1,3},{2,0},{3,1},{4,6},{5,7},{6,4},{7,5}} | collective-permute-start | bytes 6291464 | tf_op jit(solution)/shard_map/ppermute | solution.py:321
  1114.7 177.7 %collective-permute-start.7 = (bf16[256,4096]{1,0:T(8,128)(2,1)}, bf16[256,4096]{1,0:T(8,128)(2,1)}, u32[]{:S(2)}, u32[]{:S(2)}) collective-permute-start(bf16[256,4096]{1,0:T(8,128)(2,1)} %get-tuple-element.78), channel_id=1, source_target_pairs={{0,6},{1,7},{2,4},{3,5},{4,2},{5,3},{6,0},{7,1}} | collective-permute-start | bytes 6291464 | tf_op jit(solution)/shard_map/ppermute | solution.py:321
  1158.2 134.9 %collective-permute-start.6 = (bf16[256,4096]{1,0:T(8,128)(2,1)}, bf16[256,4096]{1,0:T(8,128)(2,1)}, u32[]{:S(2)}, u32[]{:S(2)}) collective-permute-start(bf16[256,4096]{1,0:T(8,128)(2,1)} %get-tuple-element.79), channel_id=1, source_target_pairs={{0,4},{1,5},{2,6},{3,7},{4,0},{5,1},{6,2},{7,3}} | collective-permute-start | bytes 6291464 | tf_op jit(solution)/shard_map/ppermute | solution.py:321
  (7 other events, 19.3 us)
Sparse Core Ops, SparseCore 0:
  12.7 87.0 all-gather.10
  101.6 84.2 all-gather.8
  187.7 84.1 all-gather.12
  273.6 84.2 all-gather.14
